TPU v7x, 32 devices: a whole 2x2x4 slice. The times are simulated.
32 devices in a mesh: dp: 16 (over z, y, core), rep: 2 (over x).
Axes of the slice: x: 2, y: 2, z: 4, core: 2. Of those that a mesh axis runs over, the one named last changes fastest.
Arguments:
- q_hidden: bfloat16 [2, 16, 128, 768], P('rep', 'dp'), may hold values from -8 to 8
- p_hidden: bfloat16 [2, 16, 128, 768], P('rep', 'dp'), may hold values from -8 to 8
- w_up: bfloat16 [1536, 768], replicated, may hold values from -0.21875 to 0.21875
- w_down: bfloat16 [1536, 768], replicated, may hold values from -0.15625 to 0.15625
- pos_index: int32 [2, 16], P('rep', 'dp'), may hold values from 0 to 15
- hard_index: int32 [2, 16, 2], P('rep', 'dp'), may hold values from 0 to 15
Outputs:
- w_up_grad: float32 [1536, 768], P(('dp', 'rep'))
- mean_loss: float32 [], replicated
All inputs are finite; a program needn't handle non-finite values.
Results may differ from a plain program's by a relative error of at most 0.008.
Values may be sent and summed in bfloat16 or wider, within the bound.
A program may use at most 64 MiB of HBM per device.

v0:
```python
import functools
import math

import jax
import jax.numpy as jnp
from jax import lax
from jax.experimental import pallas as pl
from jax.experimental.pallas import tpu as pltpu
from jax.sharding import PartitionSpec as P

norm_eps = 1e-06
HARD_BOOST = 1.5
MESH = pl.DeviceIdType.MESH
LANES = 128
ROW_TILE = 16
F32 = jnp.float32
BF16 = jnp.bfloat16


def dot_nt(left, right):
    return lax.dot_general(
        left, right, (((1,), (1,)), ((), ())), preferred_element_type=F32
    )


def phi(values):
    return 0.5 * (1.0 + lax.erf(values * (1.0 / math.sqrt(2.0))))


def gelu_slope(values):
    bell = jnp.exp(-0.5 * values * values) * (1.0 / math.sqrt(2.0 * math.pi))
    return phi(values) + values * bell


def loop(count, body):
    if count <= 16:
        for step in range(count):
            body(step)
    else:
        lax.fori_loop(0, count, lambda step, carry: (body(step), carry)[1], 0)


def kernel(
    dp, rep, pairs, length, hard,
    q_ref, p_ref, up_ref, down_ref, pos_ref, hard_ref,
    out_ref, loss_ref,
    up, down, tokens, hidden, slope, normed, inv_scale, grad_low, slots, index_slots, every,
    index_rows, gp_send, gp_recv, halves, kept, y_out, y_in, z_out, z_in, losses,
    pos_smem, hard_smem, t_sem, w_sem, x_send, x_recv, f_send, f_recv, i_send, i_recv, e_send, e_recv,
    l_send, l_recv, g_send, g_recv, y_send, y_recv, z_send, z_recv,
):
    depth = dp // 4
    members = 2 * rep
    seqs = 2 * pairs
    count = seqs * length
    features = tokens.shape[-1]
    rows = up.shape[-2]
    chunk = members * 2 * rows
    strips = rows // ROW_TILE
    padded = every.shape[0]
    me = lax.axis_index("dp")
    my_rep = lax.axis_index("rep")
    core = lax.rem(me, 2)
    side = lax.rem(me // 2, 2)
    layer = me // 4
    member = core * rep + my_rep
    partner = me + 1 - 2 * core

    def remote(src, dst, send, recv, device):
        return pltpu.make_async_remote_copy(
            src_ref=src, dst_ref=dst, send_sem=send, recv_sem=recv,
            device_id=device, device_id_type=MESH,
        )

    def ahead(step):
        return lax.rem(me + step, dp)

    def behind(step):
        return lax.rem(me + dp - step, dp)

    def rep_ahead(step):
        return lax.rem(my_rep + step, rep)

    def rep_behind(step):
        return lax.rem(my_rep + rep - step, rep)

    half = pairs * length
    load_q = pltpu.make_async_copy(q_ref, tokens.at[member, pl.ds(0, half)], t_sem.at[0])
    load_p = pltpu.make_async_copy(p_ref, tokens.at[member, pl.ds(half, half)], t_sem.at[1])
    load_q.start()
    load_p.start()
    load_pos = pltpu.make_async_copy(pos_ref, pos_smem, t_sem.at[2])
    load_hard = pltpu.make_async_copy(hard_ref, hard_smem, t_sem.at[3])

    def load(which, step, part):
        ref, buffer = ((up_ref, up), (down_ref, down))[which]
        return pltpu.make_async_copy(
            ref.at[step, part], buffer.at[step, :, part], w_sem.at[which, step]
        )

    def load_chunk(step):
        for which in range(2):
            for part in range(2):
                load(which, step, part).start()

    loop(depth, load_chunk)
    load_pos.start()
    load_hard.start()

    barrier = pltpu.get_barrier_semaphore()

    def greet(step):
        pl.semaphore_signal(
            barrier, inc=1, device_id=(ahead(step + 1), my_rep), device_id_type=MESH
        )

    loop(dp - 1, greet)
    for step in range(1, rep):
        other = rep_ahead(step)
        pl.semaphore_signal(barrier, inc=1, device_id=(me, other), device_id_type=MESH)
        pl.semaphore_signal(barrier, inc=1, device_id=(partner, other), device_id_type=MESH)

    every[...] = jnp.zeros_like(every)
    index_rows[...] = jnp.full(index_rows.shape, -1, jnp.int32)

    load_q.wait()
    load_p.wait()
    own = tokens[member]

    def wait_weights(which, step):
        buffer = (up, down)[which].at[step]
        pltpu.make_async_copy(buffer, buffer, w_sem.at[which, step]).wait()

    def forward(step):
        wait_weights(0, step)
        pre = dot_nt(own, up[step].reshape(chunk, features))
        columns = pl.ds(pl.multiple_of(step * chunk, chunk), chunk)
        hidden[:, columns] = (pre * phi(pre)).astype(BF16)

    forward(0)
    load_pos.wait()
    load_hard.wait()
    row_ids = lax.broadcasted_iota(jnp.int32, (seqs, LANES), 0)
    lane_ids = lax.broadcasted_iota(jnp.int32, (seqs, LANES), 1)
    message = jnp.full((seqs, LANES), -1, jnp.int32)
    for row in range(pairs):
        message = jnp.where((row_ids == row) & (lane_ids == 0), pos_smem[0, row], message)
        for pick in range(hard):
            message = jnp.where(
                (row_ids == row) & (lane_ids == 1 + pick), hard_smem[row, pick], message
            )
    index_slots[me] = message
    pl.semaphore_wait(barrier, dp - 1 + 2 * (rep - 1))

    def x_copy(step):
        if step == 0:
            device = (partner, my_rep)
        else:
            device = (me, rep_ahead(step))
        return remote(
            tokens.at[member], tokens.at[member], x_send.at[step], x_recv.at[step], device
        )

    for step in range(rep - 1, -1, -1):
        x_copy(step).start()

    def index_copy(step):
        return remote(
            index_slots.at[me], index_slots.at[me], i_send.at[0], i_recv.at[0],
            (ahead(step + 1), my_rep),
        )

    loop(dp - 1, lambda step: index_copy(step).start())

    loop(depth - 1, lambda step: forward(step + 1))
    loop(depth, lambda step: wait_weights(1, step))
    summed = own.astype(F32) + jnp.dot(
        hidden[...], down[...].reshape(depth * chunk, features), preferred_element_type=F32
    )

    means = []
    for seq in range(seqs):
        block = summed[seq * length:(seq + 1) * length]
        centred = block - jnp.mean(block, -1, keepdims=True)
        scale = lax.rsqrt(jnp.mean(centred * centred, -1, keepdims=True) + norm_eps)
        unit = centred * scale
        inv_scale[pl.ds(seq * length, length), :] = scale
        normed[pl.ds(seq * length, length), :] = unit
        means.append(jnp.mean(unit, 0, keepdims=True))
    slots[me] = jnp.concatenate(means, 0).astype(BF16)

    def embed_copy(step):
        return remote(
            slots.at[me], slots.at[me], e_send.at[0], e_recv.at[0],
            (ahead(step + 1), my_rep),
        )

    loop(dp - 1, lambda step: embed_copy(step).start())

    def keep_slope(step):
        pre = dot_nt(up[step].reshape(chunk, features), own)
        bell = jnp.exp(-0.5 * pre * pre) * (1.0 / math.sqrt(2.0 * math.pi))
        slope[step] = phi(pre) + pre * bell

    loop(depth, keep_slope)

    def all_indices():
        landed = index_slots.at[pl.ds(0, dp - 1)]
        return remote(landed, landed, i_send.at[0], i_recv.at[0], (me, my_rep))

    def all_embeds():
        landed = slots.at[pl.ds(0, dp - 1)]
        return remote(landed, landed, e_send.at[0], e_recv.at[0], (me, my_rep))

    all_indices().wait_recv()
    all_embeds().wait_recv()
    for slot in range(dp):
        every[slot * seqs:(slot + 1) * seqs, :] = slots[slot].astype(F32)
        index_rows[slot * seqs:(slot + 1) * seqs, :] = index_slots[slot]

    embeds = every[...].astype(BF16)
    scores = dot_nt(embeds, embeds)
    row = lax.broadcasted_iota(jnp.int32, (padded, padded), 0)
    column = lax.broadcasted_iota(jnp.int32, (padded, padded), 1)
    row_place = lax.rem(row, seqs)
    column_place = lax.rem(column, seqs)
    valid = (
        (row < dp * seqs) & (row_place < pairs) & (column < dp * seqs) & (column_place >= pairs)
    )
    passage = (column // seqs) * pairs + column_place - pairs
    indices = index_rows[...]
    target = valid & (passage == indices[:, 0:1])
    is_hard = passage == indices[:, 1:2]
    for pick in range(1, hard):
        is_hard = is_hard | (passage == indices[:, 1 + pick:2 + pick])
    logits = scores + jnp.where(is_hard, HARD_BOOST, 0.0)
    row_max = jnp.max(jnp.where(valid, logits, -1e30), -1, keepdims=True)
    powers = jnp.where(valid, jnp.exp(jnp.where(valid, logits - row_max, 0.0)), 0.0)
    powers_sum = jnp.sum(powers, -1, keepdims=True)
    log_total = row_max + jnp.log(jnp.where(powers_sum > 0.0, powers_sum, 1.0))
    picked = jnp.sum(jnp.where(target, logits, 0.0), -1, keepdims=True)
    weights = jnp.where(
        valid,
        jnp.exp(jnp.where(valid, logits - log_total, 0.0)) - jnp.where(target, 1.0, 0.0),
        0.0,
    )
    both = weights + weights.T
    own_weights = [
        jnp.sum(jnp.where(row == me * seqs + seq, both, 0.0), 0, keepdims=True)
        for seq in range(seqs)
    ]
    own_weights = jnp.concatenate(own_weights, 0).astype(BF16)
    d_own = jnp.dot(own_weights, embeds, preferred_element_type=F32) * (1.0 / length)
    row_one = lax.broadcasted_iota(jnp.int32, (padded, 1), 0)
    counted = (row_one < dp * seqs) & (lax.rem(row_one, seqs) < pairs)
    loss = jnp.sum(jnp.where(counted, log_total - picked, 0.0), 0, keepdims=True)
    losses[my_rep] = jnp.broadcast_to(loss, (1, LANES))

    def loss_copy(step):
        return remote(
            losses.at[my_rep], losses.at[my_rep], l_send.at[step], l_recv.at[step],
            (me, rep_ahead(step)),
        )

    for step in range(1, rep):
        loss_copy(step).start()

    for seq in range(seqs):
        place = pl.ds(seq * length, length)
        grad = d_own[seq:seq + 1]
        unit = normed[place, :]
        grad_low[place, :] = (
            inv_scale[place, :]
            * (
                grad
                - jnp.mean(grad, -1, keepdims=True)
                - unit * jnp.mean(grad * unit, -1, keepdims=True)
            )
        ).astype(BF16)

    def turn(step):
        own_turn = (step + 1) // depth
        upper = (2 * layer) // depth
        mirrored = upper * layer + (1 - upper) * (depth - 1 - layer)
        place = step + (step - mirrored + depth) // depth
        place = upper * place + (1 - upper) * (depth - 1 - place)
        return own_turn * layer + (1 - own_turn) * place

    def strip(sub):
        return pl.ds(sub * ROW_TILE, ROW_TILE)

    def g_copy(step, sub, jump):
        now = turn(step)
        target_member = lax.rem(member + jump, members)
        return remote(
            gp_send.at[now, target_member, :, strip(sub)],
            gp_recv.at[now, member, :, strip(sub)],
            g_send.at[0], g_recv.at[now, sub],
            (me - core + target_member // rep, lax.rem(target_member, rep)),
        )

    def backward(step):
        now = turn(step)
        grad_hidden = dot_nt(down[now].reshape(chunk, features), grad_low[...])
        grad_pre = (grad_hidden * slope[now]).astype(BF16)
        gp_send[now] = grad_pre.reshape(members, 2, rows, count)
        gp_recv[now, member] = gp_send[now, member]

    def send_grads(step):
        for sub in range(strips):
            for jump in range(1, members):
                g_copy(step, sub, jump).start()

    backward(0)
    send_grads(0)
    loop(depth - 1, lambda step: backward(step + 1))

    for step in range(1, rep):
        slot = core * rep + rep_behind(step)
        remote(
            tokens.at[slot], tokens.at[slot], x_send.at[step], x_recv.at[step],
            (me, rep_behind(step)),
        ).wait_recv()
        remote(
            tokens.at[slot], tokens.at[slot], f_send.at[step], f_recv.at[step],
            (partner, my_rep),
        ).start()
    loop(depth - 1, lambda step: send_grads(step + 1))
    slot = (1 - core) * rep + my_rep
    remote(
        tokens.at[slot], tokens.at[slot], x_send.at[0], x_recv.at[0], (partner, my_rep)
    ).wait_recv()
    for step in range(1, rep):
        slot = (1 - core) * rep + rep_behind(step)
        remote(
            tokens.at[slot], tokens.at[slot], f_send.at[step], f_recv.at[step],
            (partner, my_rep),
        ).wait_recv()

    def y_copy(now, sub):
        return remote(
            y_out.at[now, strip(sub)], y_in.at[now, strip(sub)],
            y_send.at[0], y_recv.at[now, sub],
            (me + 2 - 4 * side, my_rep),
        )

    def z_copy(now, sub):
        return remote(
            z_out.at[now, strip(sub)], z_in.at[layer, strip(sub)],
            z_send.at[0], z_recv.at[0],
            (now * 4 + side * 2 + core, my_rep),
        )

    def place_of(index):
        if strips == 1:
            return turn(index), 0
        return turn(index // strips), index % strips

    def product(index):
        now, sub = place_of(index)
        landed = gp_recv.at[now, pl.ds(0, members - 1), :, strip(sub)]
        remote(landed, landed, g_send.at[0], g_recv.at[now, sub], (me, my_rep)).wait_recv()
        total = None
        for part in range(members):
            term = jnp.dot(
                gp_recv[now, part, :, strip(sub), :].reshape(2 * ROW_TILE, count), tokens[part],
                preferred_element_type=F32,
            )
            total = term if total is None else total + term
        halves[...] = total.reshape(2, ROW_TILE, features)
        kept[now, strip(sub), :] = halves[side]
        y_out[now, strip(sub), :] = halves[1 - side].astype(BF16)
        y_copy(now, sub).start()

    def pass_on(index, last):
        now, sub = place_of(index)
        y_copy(now, sub).wait_recv()
        total = kept[now, strip(sub), :] + y_in[now, strip(sub), :].astype(F32)
        if last:
            out_ref[strip(sub), :] = total
        else:
            z_out[now, strip(sub), :] = total.astype(BF16)
            z_copy(now, sub).start()

    steps = depth * strips
    lag = 3
    moved = steps - strips
    for index in range(lag):
        product(index)

    def both_stages(index):
        product(index + lag)
        pass_on(index, False)

    paired = min(steps - lag, moved)
    loop(paired, both_stages)
    for index in range(paired, moved):
        pass_on(index, False)
    for index in range(paired + lag, steps):
        product(index)
    for index in range(moved, steps):
        pass_on(index, True)

    def all_layers():
        landed = z_in.at[pl.ds(0, depth - 1)]
        return remote(landed, landed, z_send.at[0], z_recv.at[0], (me, my_rep))

    all_layers().wait_recv()

    def collect(step):
        source = lax.rem(layer + depth - 1 - step, depth)
        out_ref[...] += z_in[source].astype(F32)

    loop(depth - 1, collect)

    for step in range(1, rep):
        source = rep_behind(step)
        remote(
            losses.at[source], losses.at[source], l_send.at[step], l_recv.at[step],
            (me, source),
        ).wait_recv()
    loss_total = losses[0]
    for part in range(1, rep):
        loss_total = loss_total + losses[part]
    loss_ref[...] = loss_total[:, 0:1] * (1.0 / (dp * pairs * rep))

    all_indices().wait_send()
    all_embeds().wait_send()
    for step in range(rep):
        x_copy(step).wait_send()
    for step in range(1, rep):
        loss_copy(step).wait_send()
        slot = core * rep + rep_behind(step)
        remote(
            tokens.at[slot], tokens.at[slot], f_send.at[step], f_recv.at[step],
            (partner, my_rep),
        ).wait_send()

    sent = gp_send.at[:, pl.ds(0, members - 1)]
    remote(sent, sent, g_send.at[0], g_recv.at[0, 0], (me, my_rep)).wait_send()
    remote(y_out, y_in, y_send.at[0], y_recv.at[0, 0], (me, my_rep)).wait_send()
    all_layers().wait_send()


def shards(dp, rep, q_hidden, p_hidden, w_up, w_down, pos_index, hard_index):
    pairs, length, features = q_hidden.shape[1:]
    hard = hard_index.shape[-1]
    hidden_units = w_up.shape[0]
    own_rows = hidden_units // (dp * rep)
    rows = -(-own_rows // ROW_TILE) * ROW_TILE
    depth = dp // 4
    members = 2 * rep
    strips = rows // ROW_TILE
    seqs = 2 * pairs
    count = seqs * length
    padded = -(-dp * seqs // LANES) * LANES
    chunk = members * 2 * rows

    def arrange(weight):
        blocks = weight.reshape(dp * rep, own_rows, features)
        if rows != own_rows:
            blocks = jnp.pad(blocks, ((0, 0), (0, rows - own_rows), (0, 0)))
        return blocks.reshape(depth, 2, members, rows, features)

    dma = pltpu.SemaphoreType.DMA
    hbm = pl.BlockSpec(memory_space=pl.ANY)
    fixed = pl.BlockSpec(memory_space=pltpu.HBM)
    vmem = pl.BlockSpec(memory_space=pltpu.VMEM)
    grad, loss = pl.pallas_call(
        functools.partial(kernel, dp, rep, pairs, length, hard),
        name="gradcache_step",
        out_shape=(
            pltpu.VMEM((rows, features), F32),
            pltpu.VMEM((1, 1), F32),
        ),
        in_specs=[hbm] * 4 + [fixed] * 2,
        out_specs=(vmem, vmem),
        scratch_shapes=[
            pltpu.VMEM((depth, members, 2, rows, features), BF16),
            pltpu.VMEM((depth, members, 2, rows, features), BF16),
            pltpu.VMEM((members, count, features), BF16),
            pltpu.VMEM((count, depth * chunk), BF16),
            pltpu.VMEM((depth, chunk, count), F32),
            pltpu.VMEM((count, features), F32),
            pltpu.VMEM((count, 1), F32),
            pltpu.VMEM((count, features), BF16),
            pltpu.VMEM((dp, seqs, features), BF16),
            pltpu.VMEM((dp, seqs, LANES), jnp.int32),
            pltpu.VMEM((padded, features), F32),
            pltpu.VMEM((padded, LANES), jnp.int32),
            pltpu.VMEM((depth, members, 2, rows, count), BF16),
            pltpu.VMEM((depth, members, 2, rows, count), BF16),
            pltpu.VMEM((2, ROW_TILE, features), F32),
            pltpu.VMEM((depth, rows, features), F32),
            pltpu.VMEM((depth, rows, features), BF16),
            pltpu.VMEM((depth, rows, features), BF16),
            pltpu.VMEM((depth, rows, features), BF16),
            pltpu.VMEM((depth, rows, features), BF16),
            pltpu.VMEM((rep, 1, LANES), F32),
            pltpu.SMEM((1, pairs), jnp.int32), pltpu.SMEM((pairs, hard), jnp.int32),
            dma((4,)), dma((2, depth)),
            dma((rep,)), dma((rep,)), dma((rep,)), dma((rep,)),
            dma((1,)), dma((1,)), dma((1,)), dma((1,)),
            dma((rep,)), dma((rep,)),
            dma((1,)), dma((depth, strips)), dma((1,)), dma((depth, strips)),
            dma((1,)), dma((1,)),
        ],
        compiler_params=pltpu.CompilerParams(
            collective_id=0, has_side_effects=True, vmem_limit_bytes=60 * 1024 * 1024
        ),
    )(
        q_hidden.reshape(pairs * length, features),
        p_hidden.reshape(pairs * length, features),
        arrange(w_up),
        arrange(w_down),
        pos_index.reshape(1, pairs),
        hard_index.reshape(pairs, hard),
    )
    return grad[:own_rows], loss.reshape(())


def solution(mesh):
    return jax.shard_map(
        functools.partial(shards, mesh.shape["dp"], mesh.shape["rep"]),
        mesh=mesh,
        in_specs=(
            P("rep", "dp", None, None),
            P("rep", "dp", None, None),
            P(),
            P(),
            P("rep", "dp"),
            P("rep", "dp", None),
        ),
        out_specs=(P(("dp", "rep"), None), P()),
        check_vma=False,
    )
```

profile of v0, /device:TPU:0, one launch (start us, length us, event | category | flops | bytes accessed | tf_op | source)
XLA Modules:
  0.0 33.8 jit_solution(7537002202165797362)
XLA Ops:
  1.3 30.7 %gradcache_step.1 = (f32[48,768]{1,0:T(8,128)S(1)}, f32[1,1]{1,0:T(1,128)S(1)}) custom-call(bf16[128,768]{1,0:T(8,128)(2,1)} %bitcast.8, bf16[128,768]{1,0:T(8,128)(2,1)} %bitcast.9, bf16[4,2,4,48,768]{4,3,2,1,0:T(8,128)(2,1)} %bitcast.6, bf16[4,2,4,48,768]{4,3,2,1,0:T(8,128)(2,1)} %bitcast.7, s32[1,1]{1,0:T(1,128)S(6)} %copy.12.pos_ref, s32[1,2]{1,0:T(1,128)} %bitcast.10), custom_call_target="tpu_custom_call" | custom-call | tf_op jit(solution)/shard_map/gradcache_step/pallas_call | solution.py:469
  32.0 0.7 %copy.10 = f32[48,768]{1,0:T(8,128)} copy(f32[48,768]{1,0:T(8,128)S(1)} %get-tuple-element.6) | data formatting | bytes 294912
where the time goes:
time: 34 us; the launch traced here: 33.8 us
  Pallas kernels  30.7 us (90%)
  between operations  2.45 us (7%)
  local copies, waits for them, and re-layouts  0.66 us (2%)
    pallas_call x1, Pallas kernels, shards(): pl.pallas_call(functools.partial(kernel, dp, rep, pairs, length, hard), n...  30.7 us

commit v1 on v0

--- a/solution.py
+++ b/solution.py
@@ -47,7 +47,7 @@
     up, down, tokens, hidden, slope, normed, inv_scale, grad_low, slots, index_slots, every,
     index_rows, gp_send, gp_recv, halves, kept, y_out, y_in, z_out, z_in, losses,
     pos_smem, hard_smem, t_sem, w_sem, x_send, x_recv, f_send, f_recv, i_send, i_recv, e_send, e_recv,
-    l_send, l_recv, g_send, g_recv, y_send, y_recv, z_send, z_recv,
+    l_send, l_recv, g_send, g_recv, y_send, y_recv, z_send, z_recv, below, above,
 ):
     depth = dp // 4
     members = 2 * rep
@@ -109,16 +109,59 @@
 
     barrier = pltpu.get_barrier_semaphore()
 
-    def greet(step):
+    opposite = me + 2 - 4 * side
+
+    def greet(device, group):
         pl.semaphore_signal(
-            barrier, inc=1, device_id=(ahead(step + 1), my_rep), device_id_type=MESH
-        )
-
-    loop(dp - 1, greet)
+            barrier, inc=1, device_id=(device, group), device_id_type=MESH
+        )
+
+    greet(partner, my_rep)
     for step in range(1, rep):
-        other = rep_ahead(step)
-        pl.semaphore_signal(barrier, inc=1, device_id=(me, other), device_id_type=MESH)
-        pl.semaphore_signal(barrier, inc=1, device_id=(partner, other), device_id_type=MESH)
+        greet(me, rep_ahead(step))
+        greet(partner, rep_ahead(step))
+    greet(opposite, my_rep)
+    greet(opposite + partner - me, my_rep)
+
+    @pl.when(layer + 1 < depth)
+    def greet_above():
+        greet(me + 4, my_rep)
+
+    @pl.when(layer > 0)
+    def greet_below():
+        greet(me - 4, my_rep)
+
+    def wait_near():
+        pl.semaphore_wait(
+            barrier,
+            3 + 2 * (rep - 1) + jnp.where(layer + 1 < depth, 1, 0) + jnp.where(layer > 0, 1, 0),
+        )
+
+    def hear(step):
+        @pl.when(layer >= step)
+        def from_below():
+            pl.semaphore_wait(below, 1)
+
+        @pl.when(layer + step < depth)
+        def from_above():
+            pl.semaphore_wait(above, 1)
+
+    def tell(step):
+        @pl.when((layer >= step) & (layer + 1 < depth))
+        def to_above():
+            pl.semaphore_signal(below, inc=1, device_id=(me + 4, my_rep), device_id_type=MESH)
+
+        @pl.when((layer + step < depth) & (layer > 0))
+        def to_below():
+            pl.semaphore_signal(above, inc=1, device_id=(me - 4, my_rep), device_id_type=MESH)
+
+    def spread(step):
+        hear(step)
+        if depth <= 16:
+            if step < depth - 1:
+                tell(step)
+        else:
+            pl.when(step < depth - 1)(lambda: tell(step))
 
     every[...] = jnp.zeros_like(every)
     index_rows[...] = jnp.full(index_rows.shape, -1, jnp.int32)
@@ -150,7 +193,8 @@
                 (row_ids == row) & (lane_ids == 1 + pick), hard_smem[row, pick], message
             )
     index_slots[me] = message
-    pl.semaphore_wait(barrier, dp - 1 + 2 * (rep - 1))
+    wait_near()
+    tell(0)
 
     def x_copy(step):
         if step == 0:
@@ -170,9 +214,12 @@
             (ahead(step + 1), my_rep),
         )
 
+    def forward_and_spread(step):
+        forward(step + 1)
+        spread(step + 1)
+
+    loop(depth - 1, forward_and_spread)
     loop(dp - 1, lambda step: index_copy(step).start())
-
-    loop(depth - 1, lambda step: forward(step + 1))
     loop(depth, lambda step: wait_weights(1, step))
     summed = own.astype(F32) + jnp.dot(
         hidden[...], down[...].reshape(depth * chunk, features), preferred_element_type=F32
@@ -504,6 +551,7 @@
             dma((rep,)), dma((rep,)),
             dma((1,)), dma((depth, strips)), dma((1,)), dma((depth, strips)),
             dma((1,)), dma((1,)),
+            pltpu.SemaphoreType.REGULAR, pltpu.SemaphoreType.REGULAR,
         ],
         compiler_params=pltpu.CompilerParams(
             collective_id=0, has_side_effects=True, vmem_limit_bytes=60 * 1024 * 1024

time: 34 us -> 35.1 us (1.032)
  Pallas kernels: 30.7 us -> 31.8 us
    pallas_call x1, Pallas kernels: 30.7 us -> 31.8 us  [shards(): pl.pallas_call(functools.partial(kernel, dp, rep, pairs, length, hard), n...]
where the time goes in v1:
time: 35.1 us; the launch traced here: 34.9 us
  Pallas kernels  31.8 us (91%)
  between operations  2.45 us (7%)
  local copies, waits for them, and re-layouts  0.66 us (2%)
    pallas_call x1, Pallas kernels, shards(): pl.pallas_call(functools.partial(kernel, dp, rep, pairs, length, hard), n...  31.8 us

profile of v1, /device:TPU:0, one launch (start us, length us, event | category | flops | bytes accessed | tf_op | source)
XLA Modules:
  0.0 34.9 jit_solution(14639547409326086421)
XLA Ops:
  1.3 31.8 %gradcache_step.1 = (f32[48,768]{1,0:T(8,128)S(1)}, f32[1,1]{1,0:T(1,128)S(1)}) custom-call(bf16[128,768]{1,0:T(8,128)(2,1)} %bitcast.8, bf16[128,768]{1,0:T(8,128)(2,1)} %bitcast.9, bf16[4,2,4,48,768]{4,3,2,1,0:T(8,128)(2,1)} %bitcast.6, bf16[4,2,4,48,768]{4,3,2,1,0:T(8,128)(2,1)} %bitcast.7, s32[1,1]{1,0:T(1,128)S(6)} %copy.12.pos_ref, s32[1,2]{1,0:T(1,128)} %bitcast.10), custom_call_target="tpu_custom_call" | custom-call | tf_op jit(solution)/shard_map/gradcache_step/pallas_call | solution.py:516
  33.1 0.7 %copy.10 = f32[48,768]{1,0:T(8,128)} copy(f32[48,768]{1,0:T(8,128)S(1)} %get-tuple-element.6) | data formatting | bytes 294912

commit v2 on v0

v2 whole, which is shorter than its diff:
```python
import functools
import math

import jax
import jax.numpy as jnp
from jax import lax
from jax.experimental import pallas as pl
from jax.experimental.pallas import tpu as pltpu
from jax.sharding import PartitionSpec as P

norm_eps = 1e-06
HARD_BOOST = 1.5
MESH = pl.DeviceIdType.MESH
LANES = 128
ROW_TILE = 16
LAGS = (6, 3)
F32 = jnp.float32
BF16 = jnp.bfloat16


def dot_nt(left, right):
    return lax.dot_general(
        left, right, (((1,), (1,)), ((), ())), preferred_element_type=F32
    )


def phi(values):
    return 0.5 * (1.0 + lax.erf(values * (1.0 / math.sqrt(2.0))))


def loop(count, body):
    if count <= 16:
        for step in range(count):
            body(step)
    else:
        lax.fori_loop(0, count, lambda step, carry: (body(step), carry)[1], 0)


def pipeline(tasks):
    cuts = sorted({edge - offset for _, first, last, offset in tasks for edge in (first, last)})
    for low, high in zip(cuts[:-1], cuts[1:]):
        active = [
            (body, offset) for body, first, last, offset in tasks
            if first <= low + offset and high + offset <= last
        ]

        def step_body(step, low=low, active=active):
            for body, offset in active:
                body(low + step + offset)

        loop(high - low, step_body)


def kernel(
    dp, pairs, length, hard,
    q_ref, p_ref, up_ref, down_ref, pos_ref, hard_ref,
    out_ref, loss_ref,
    up, down, tokens, hidden, normed, scales, slope, mixed, grads, slots, index_slots, every, index_rows,
    first_out, first_in, first_kept, second_out, second_in, second_kept, z_out, z_in, losses,
    pos_smem, hard_smem, t_sem, w_sem, d_send, d_recv, i_send, i_recv, e_send, e_recv,
    l_send, l_recv, first_send, first_recv, second_send, second_recv, z_send, z_recv,
):
    depth = dp // 4
    seqs = 2 * pairs
    count = seqs * length
    features = tokens.shape[-1]
    half = features // 2
    rows = up.shape[-2]
    block = 4 * rows
    chunk = 8 * rows
    strips = rows // ROW_TILE
    padded = every.shape[0]
    me = lax.axis_index("dp")
    my_rep = lax.axis_index("rep")
    other_rep = 1 - my_rep
    core = lax.rem(me, 2)
    side = lax.rem(me // 2, 2)
    layer = me // 4
    partner = me + 1 - 2 * core
    opposite = me + 2 - 4 * side

    def remote(src, dst, send, recv, device):
        return pltpu.make_async_remote_copy(
            src_ref=src, dst_ref=dst, send_sem=send, recv_sem=recv,
            device_id=device, device_id_type=MESH,
        )

    def ahead(step):
        return lax.rem(me + step, dp)

    half_count = pairs * length
    load_q = pltpu.make_async_copy(q_ref, tokens.at[core, pl.ds(0, half_count)], t_sem.at[0])
    load_p = pltpu.make_async_copy(p_ref, tokens.at[core, pl.ds(half_count, half_count)], t_sem.at[1])
    load_q.start()
    load_p.start()
    load_pos = pltpu.make_async_copy(pos_ref, pos_smem, t_sem.at[2])
    load_hard = pltpu.make_async_copy(hard_ref, hard_smem, t_sem.at[3])

    def load(which, step):
        ref, buffer = ((up_ref, up), (down_ref, down))[which]
        return pltpu.make_async_copy(ref.at[step], buffer.at[step], w_sem.at[which, step])

    loop(depth, lambda step: load(0, step).start())
    loop(depth, lambda step: load(1, step).start())
    load_pos.start()
    load_hard.start()

    barrier = pltpu.get_barrier_semaphore()

    def greet(step):
        pl.semaphore_signal(
            barrier, inc=1, device_id=(ahead(step + 1), my_rep), device_id_type=MESH
        )

    loop(dp - 1, greet)
    pl.semaphore_signal(barrier, inc=1, device_id=(me, other_rep), device_id_type=MESH)

    every[...] = jnp.zeros_like(every)
    index_rows[...] = jnp.full(index_rows.shape, -1, jnp.int32)

    load_q.wait()
    load_p.wait()
    own = tokens[core]

    def forward(step):
        load(0, step).wait()
        pre = dot_nt(own, up[step].reshape(chunk, features))
        columns = pl.ds(pl.multiple_of(step * chunk, chunk), chunk)
        hidden[:, columns] = (pre * phi(pre)).astype(BF16)

    loop(depth, forward)
    loop(depth, lambda step: load(1, step).wait())
    summed = own.astype(F32) + jnp.dot(
        hidden[...], down[...].reshape(depth * chunk, features), preferred_element_type=F32
    )

    means = []
    for seq in range(seqs):
        place = pl.ds(seq * length, length)
        part = summed[seq * length:(seq + 1) * length]
        centred = part - jnp.mean(part, -1, keepdims=True)
        scale = lax.rsqrt(jnp.mean(centred * centred, -1, keepdims=True) + norm_eps)
        unit = centred * scale
        normed[core, place, :] = unit.astype(BF16)
        scales[core, :, place] = jnp.broadcast_to(scale, (length, LANES)).T[0:8]
        means.append(jnp.mean(unit, 0, keepdims=True))
    slots[me] = jnp.concatenate(means, 0).astype(BF16)

    load_pos.wait()
    load_hard.wait()
    row_ids = lax.broadcasted_iota(jnp.int32, (seqs, LANES), 0)
    lane_ids = lax.broadcasted_iota(jnp.int32, (seqs, LANES), 1)
    message = jnp.full((seqs, LANES), -1, jnp.int32)
    for row in range(pairs):
        message = jnp.where((row_ids == row) & (lane_ids == 0), pos_smem[0, row], message)
        for pick in range(hard):
            message = jnp.where(
                (row_ids == row) & (lane_ids == 1 + pick), hard_smem[row, pick], message
            )
    index_slots[me] = message

    pl.semaphore_wait(barrier, dp)

    def embed_copy(step):
        return remote(
            slots.at[me], slots.at[me], e_send.at[0], e_recv.at[0],
            (ahead(step + 1), my_rep),
        )

    def index_copy(step):
        return remote(
            index_slots.at[me], index_slots.at[me], i_send.at[0], i_recv.at[0],
            (ahead(step + 1), my_rep),
        )

    loop(dp - 1, lambda step: embed_copy(step).start())
    loop(dp - 1, lambda step: index_copy(step).start())

    def twin_copy(which, slot):
        ref = (tokens, normed, scales)[which].at[slot]
        return remote(ref, ref, d_send.at[which], d_recv.at[which], (partner, my_rep))

    for which in range(3):
        twin_copy(which, core).start()

    def mix(step, slot):
        pre = dot_nt(up[step, :, core].reshape(block, features), tokens[slot])
        bell = jnp.exp(-0.5 * pre * pre) * (1.0 / math.sqrt(2.0 * math.pi))
        slope[slot, step] = (phi(pre) + pre * bell) * scales[slot][0:1]
        mixed[slot, step] = dot_nt(down[step, :, core].reshape(block, features), normed[slot])

    loop(depth, lambda step: mix(step, core))
    for which in range(3):
        twin_copy(which, 1 - core).wait_recv()
    loop(depth, lambda step: mix(step, 1 - core))

    def all_indices():
        landed = index_slots.at[pl.ds(0, dp - 1)]
        return remote(landed, landed, i_send.at[0], i_recv.at[0], (me, my_rep))

    def all_embeds():
        landed = slots.at[pl.ds(0, dp - 1)]
        return remote(landed, landed, e_send.at[0], e_recv.at[0], (me, my_rep))

    all_indices().wait_recv()
    all_embeds().wait_recv()
    for slot in range(dp):
        every[slot * seqs:(slot + 1) * seqs, :] = slots[slot].astype(F32)
        index_rows[slot * seqs:(slot + 1) * seqs, :] = index_slots[slot]

    embeds = every[...].astype(BF16)
    scores = dot_nt(embeds, embeds)
    row = lax.broadcasted_iota(jnp.int32, (padded, padded), 0)
    column = lax.broadcasted_iota(jnp.int32, (padded, padded), 1)
    row_place = lax.rem(row, seqs)
    column_place = lax.rem(column, seqs)
    valid = (
        (row < dp * seqs) & (row_place < pairs) & (column < dp * seqs) & (column_place >= pairs)
    )
    passage = (column // seqs) * pairs + column_place - pairs
    indices = index_rows[...]
    target = valid & (passage == indices[:, 0:1])
    is_hard = passage == indices[:, 1:2]
    for pick in range(1, hard):
        is_hard = is_hard | (passage == indices[:, 1 + pick:2 + pick])
    logits = scores + jnp.where(is_hard, HARD_BOOST, 0.0)
    row_max = jnp.max(jnp.where(valid, logits, -1e30), -1, keepdims=True)
    powers = jnp.where(valid, jnp.exp(jnp.where(valid, logits - row_max, 0.0)), 0.0)
    powers_sum = jnp.sum(powers, -1, keepdims=True)
    log_total = row_max + jnp.log(jnp.where(powers_sum > 0.0, powers_sum, 1.0))
    picked = jnp.sum(jnp.where(target, logits, 0.0), -1, keepdims=True)
    weights = jnp.where(
        valid,
        jnp.exp(jnp.where(valid, logits - log_total, 0.0)) - jnp.where(target, 1.0, 0.0),
        0.0,
    )
    both = weights + weights.T
    chip_seqs = 2 * seqs
    first_row = (me - core) * seqs
    chip_weights = jnp.concatenate(
        [
            jnp.sum(jnp.where(row == first_row + seq, both, 0.0), 0, keepdims=True)
            for seq in range(chip_seqs)
        ]
        + [jnp.zeros((-chip_seqs % 8, padded), F32)] * (1 if chip_seqs % 8 else 0),
        0,
    ).astype(BF16)
    d_chip = jnp.dot(chip_weights, embeds, preferred_element_type=F32) * (1.0 / length)
    d_low = (d_chip - jnp.mean(d_chip, -1, keepdims=True)).astype(BF16)
    aligned = [dot_nt(d_low, normed[slot]) * (1.0 / features) for slot in range(2)]
    row_one = lax.broadcasted_iota(jnp.int32, (padded, 1), 0)
    counted = (row_one < dp * seqs) & (lax.rem(row_one, seqs) < pairs)
    loss = jnp.sum(jnp.where(counted, log_total - picked, 0.0), 0, keepdims=True)
    losses[my_rep] = jnp.broadcast_to(loss, (1, LANES))

    def loss_copy(group):
        return remote(
            losses.at[group], losses.at[group], l_send.at[0], l_recv.at[0], (me, other_rep)
        )

    def strip(sub):
        return pl.ds(sub * ROW_TILE, ROW_TILE)

    def turn(step):
        own_turn = (step + 1) // depth
        upper = (2 * layer) // depth
        mirrored = upper * layer + (1 - upper) * (depth - 1 - layer)
        place = step + (step - mirrored + depth) // depth
        place = upper * place + (1 - upper) * (depth - 1 - place)
        return own_turn * layer + (1 - own_turn) * place

    def place_of(index):
        if strips == 1:
            return turn(index), 0
        return turn(index // strips), index % strips

    low, high = slice(0, half), slice(half, features)

    def backward(step):
        now = turn(step)
        spread = dot_nt(down[now, :, core].reshape(block, features), d_low)
        for slot in range(2):
            for seq in range(seqs):
                which = slot * seqs + seq
                place = slice(seq * length, (seq + 1) * length)
                grads[:, slot * count + seq * length:slot * count + (seq + 1) * length] = (
                    slope[slot, now, :, place]
                    * (
                        spread[:, which:which + 1]
                        - aligned[slot][which:which + 1, place] * mixed[slot, now, :, place]
                    )
                ).astype(BF16)
        total = jnp.dot(
            grads[...], tokens[...].reshape(2 * count, features), preferred_element_type=F32
        ).reshape(2, 2, rows, features)
        by_side = [total[0, :, :, high], total[1, :, :, high]]
        by_rep = [total[:, 0, :, low], total[:, 1, :, low]]
        mine = (my_rep == 0)
        first_out[now, 0] = jnp.where(mine, by_rep[1], by_rep[0]).astype(BF16)
        first_kept[now, 0] = jnp.where(mine, by_rep[0], by_rep[1])
        mine = (side == 0)
        first_out[now, 1] = jnp.where(mine, by_side[1], by_side[0]).astype(BF16)
        first_kept[now, 1] = jnp.where(mine, by_side[0], by_side[1])

    across = ((me, other_rep), (opposite, my_rep))

    def first_copy(now, sub, way):
        return remote(
            first_out.at[now, way, :, strip(sub)], first_in.at[now, way, :, strip(sub)],
            first_send.at[way], first_recv.at[now, sub, way], across[way],
        )

    def second_copy(now, sub, way):
        return remote(
            second_out.at[now, way, strip(sub)], second_in.at[now, way, strip(sub)],
            second_send.at[way], second_recv.at[now, sub, way], across[1 - way],
        )

    def z_copy(now, sub):
        return remote(
            z_out.at[now, strip(sub)], z_in.at[layer, strip(sub)],
            z_send.at[0], z_recv.at[0],
            (now * 4 + side * 2 + core, my_rep),
        )

    def send_first(index):
        now, sub = place_of(index)
        for way in range(2):
            first_copy(now, sub, way).start()

    def stage_two(index):
        now, sub = place_of(index)
        for way in range(2):
            stays = (side, my_rep)[way]
            first_copy(now, sub, way).wait_recv()
            second_out[now, way, strip(sub), :] = (
                first_kept[now, way, 1 - stays, strip(sub), :]
                + first_in[now, way, 1 - stays, strip(sub), :].astype(F32)
            ).astype(BF16)
            second_copy(now, sub, way).start()
            second_kept[now, way, strip(sub), :] = (
                first_kept[now, way, stays, strip(sub), :]
                + first_in[now, way, stays, strip(sub), :].astype(F32)
            )

    def stage_three(index, last):
        now, sub = place_of(index)
        for way in range(2):
            second_copy(now, sub, way).wait_recv()
            total = second_kept[now, way, strip(sub), :] + second_in[now, way, strip(sub), :].astype(F32)
            if last:
                out_ref[strip(sub), (low, high)[way]] = total
            else:
                z_out[now, strip(sub), (low, high)[way]] = total.astype(BF16)
        if not last:
            z_copy(now, sub).start()

    steps = depth * strips
    moved = steps - strips
    lag_one, lag_two = LAGS
    early = min(depth, -(-lag_one // strips))

    def backward_and_send(step):
        backward(step)
        for sub in range(strips):
            send_first(step * strips + sub)

    loop(early, backward_and_send)
    loss_copy(my_rep).start()
    loop(depth - early, lambda step: backward(step + early))
    sent = early * strips
    pipeline([
        (send_first, sent, steps, sent),
        (stage_two, 0, steps, 0),
        (lambda index: stage_three(index, False), 0, moved, -lag_two),
        (lambda index: stage_three(index, True), moved, steps, -lag_two),
    ])

    def all_layers():
        landed = z_in.at[pl.ds(0, depth - 1)]
        return remote(landed, landed, z_send.at[0], z_recv.at[0], (opposite, my_rep))

    all_layers().wait_recv()

    def collect(step):
        source = lax.rem(layer + depth - 1 - step, depth)
        out_ref[...] += z_in[source].astype(F32)

    loop(depth - 1, collect)

    loss_copy(other_rep).wait_recv()
    loss_ref[...] = (losses[0] + losses[1])[:, 0:1] * (1.0 / (dp * pairs * 2))

    all_indices().wait_send()
    all_embeds().wait_send()
    for which in range(3):
        twin_copy(which, core).wait_send()
    loss_copy(my_rep).wait_send()
    for way in range(2):
        sent_first = first_out.at[:, way]
        remote(sent_first, sent_first, first_send.at[way], first_recv.at[0, 0, way], across[way]).wait_send()
        sent_second = second_out.at[:, way]
        remote(sent_second, sent_second, second_send.at[way], second_recv.at[0, 0, way], across[1 - way]).wait_send()
    all_layers().wait_send()


def shards(dp, rep, q_hidden, p_hidden, w_up, w_down, pos_index, hard_index):
    assert rep == 2 and dp % 4 == 0
    pairs, length, features = q_hidden.shape[1:]
    hard = hard_index.shape[-1]
    hidden_units = w_up.shape[0]
    own_rows = hidden_units // (dp * rep)
    rows = -(-own_rows // ROW_TILE) * ROW_TILE
    depth = dp // 4
    strips = rows // ROW_TILE
    seqs = 2 * pairs
    count = seqs * length
    padded = -(-dp * seqs // LANES) * LANES
    chunk = 8 * rows
    half = features // 2

    def arrange(weight):
        blocks = weight.reshape(dp * rep, own_rows, features)
        if rows != own_rows:
            blocks = jnp.pad(blocks, ((0, 0), (0, rows - own_rows), (0, 0)))
        return blocks.reshape(depth, 2, 2, 2, rows, features)

    dma = pltpu.SemaphoreType.DMA
    hbm = pl.BlockSpec(memory_space=pl.ANY)
    fixed = pl.BlockSpec(memory_space=pltpu.HBM)
    vmem = pl.BlockSpec(memory_space=pltpu.VMEM)
    grad, loss = pl.pallas_call(
        functools.partial(kernel, dp, pairs, length, hard),
        name="gradcache_step",
        out_shape=(
            pltpu.VMEM((rows, features), F32),
            pltpu.VMEM((1, 1), F32),
        ),
        in_specs=[hbm] * 4 + [fixed] * 2,
        out_specs=(vmem, vmem),
        scratch_shapes=[
            pltpu.VMEM((depth, 2, 2, 2, rows, features), BF16),
            pltpu.VMEM((depth, 2, 2, 2, rows, features), BF16),
            pltpu.VMEM((2, count, features), BF16),
            pltpu.VMEM((count, depth * chunk), BF16),
            pltpu.VMEM((2, count, features), BF16),
            pltpu.VMEM((2, 8, count), F32),
            pltpu.VMEM((2, depth, 4 * rows, count), F32),
            pltpu.VMEM((2, depth, 4 * rows, count), F32),
            pltpu.VMEM((4 * rows, 2 * count), BF16),
            pltpu.VMEM((dp, seqs, features), BF16),
            pltpu.VMEM((dp, seqs, LANES), jnp.int32),
            pltpu.VMEM((padded, features), F32),
            pltpu.VMEM((padded, LANES), jnp.int32),
            pltpu.VMEM((depth, 2, 2, rows, half), BF16),
            pltpu.VMEM((depth, 2, 2, rows, half), BF16),
            pltpu.VMEM((depth, 2, 2, rows, half), F32),
            pltpu.VMEM((depth, 2, rows, half), BF16),
            pltpu.VMEM((depth, 2, rows, half), BF16),
            pltpu.VMEM((depth, 2, rows, half), F32),
            pltpu.VMEM((depth, rows, features), BF16),
            pltpu.VMEM((depth, rows, features), BF16),
            pltpu.VMEM((2, 1, LANES), F32),
            pltpu.SMEM((1, pairs), jnp.int32), pltpu.SMEM((pairs, hard), jnp.int32),
            dma((4,)), dma((2, depth)),
            dma((3,)), dma((3,)), dma((1,)), dma((1,)), dma((1,)), dma((1,)),
            dma((1,)), dma((1,)),
            dma((2,)), dma((depth, strips, 2)), dma((2,)), dma((depth, strips, 2)),
            dma((1,)), dma((1,)),
        ],
        compiler_params=pltpu.CompilerParams(
            collective_id=0, has_side_effects=True, vmem_limit_bytes=60 * 1024 * 1024
        ),
    )(
        q_hidden.reshape(pairs * length, features),
        p_hidden.reshape(pairs * length, features),
        arrange(w_up),
        arrange(w_down),
        pos_index.reshape(1, pairs),
        hard_index.reshape(pairs, hard),
    )
    return grad[:own_rows], loss.reshape(())


def solution(mesh):
    return jax.shard_map(
        functools.partial(shards, mesh.shape["dp"], mesh.shape["rep"]),
        mesh=mesh,
        in_specs=(
            P("rep", "dp", None, None),
            P("rep", "dp", None, None),
            P(),
            P(),
            P("rep", "dp"),
            P("rep", "dp", None),
        ),
        out_specs=(P(("dp", "rep"), None), P()),
        check_vma=False,
    )
```

time: 34 us -> 33.7 us (level)
  no operation moved by 1% of the time
where the time goes in v2:
time: 33.7 us; the launch traced here: 33.5 us
  Pallas kernels  30.4 us (90%)
  between operations  2.45 us (7%)
  local copies, waits for them, and re-layouts  0.66 us (2%)
    pallas_call x1, Pallas kernels, shards(): pl.pallas_call(functools.partial(kernel, dp, pairs, length, hard), name='...  30.4 us

profile of v2, /device:TPU:0, one launch (start us, length us, event | category | flops | bytes accessed | tf_op | source)
XLA Modules:
  0.0 33.5 jit_solution(10993123032146972479)
XLA Ops:
  1.3 30.4 %gradcache_step.1 = (f32[48,768]{1,0:T(8,128)S(1)}, f32[1,1]{1,0:T(1,128)S(1)}) custom-call(bf16[128,768]{1,0:T(8,128)(2,1)} %bitcast.8, bf16[128,768]{1,0:T(8,128)(2,1)} %bitcast.9, bf16[4,2,2,2,48,768]{5,4,3,2,1,0:T(8,128)(2,1)} %bitcast.6, bf16[4,2,2,2,48,768]{5,4,3,2,1,0:T(8,128)(2,1)} %bitcast.7, s32[1,1]{1,0:T(1,128)S(6)} %copy.12.pos_ref, s32[1,2]{1,0:T(1,128)} %bitcast.10), custom_call_target="tpu_custom_call" | custom-call | tf_op jit(solution)/shard_map/gradcache_step/pallas_call | solution.py:432
  31.7 0.7 %copy.10 = f32[48,768]{1,0:T(8,128)} copy(f32[48,768]{1,0:T(8,128)S(1)} %get-tuple-element.6) | data formatting | bytes 294912

commit v3 on v2

--- a/solution.py
+++ b/solution.py
@@ -13,7 +13,7 @@
 MESH = pl.DeviceIdType.MESH
 LANES = 128
 ROW_TILE = 16
-LAGS = (6, 3)
+LAGS = (6, 5)
 F32 = jnp.float32
 BF16 = jnp.bfloat16
 
@@ -123,12 +123,13 @@
     own = tokens[core]
 
     def forward(step):
-        load(0, step).wait()
-        pre = dot_nt(own, up[step].reshape(chunk, features))
-        columns = pl.ds(pl.multiple_of(step * chunk, chunk), chunk)
+        pre = dot_nt(own, up[pl.ds(step * span, span)].reshape(span * chunk, features))
+        columns = pl.ds(pl.multiple_of(step * span * chunk, span * chunk), span * chunk)
         hidden[:, columns] = (pre * phi(pre)).astype(BF16)
 
-    loop(depth, forward)
+    span = 2 - depth % 2
+    loop(depth, lambda step: load(0, step).wait())
+    loop(depth // span, forward)
     loop(depth, lambda step: load(1, step).wait())
     summed = own.astype(F32) + jnp.dot(
         hidden[...], down[...].reshape(depth * chunk, features), preferred_element_type=F32

time: 33.7 us -> 31.9 us (0.947)
  Pallas kernels: 30.4 us -> 28.6 us
    pallas_call x1, Pallas kernels: 30.4 us -> 28.6 us  [shards(): pl.pallas_call(functools.partial(kernel, dp, pairs, length, hard), name='...]
where the time goes in v3:
time: 31.9 us; the launch traced here: 31.7 us
  Pallas kernels  28.6 us (90%)
  between operations  2.45 us (8%)
  local copies, waits for them, and re-layouts  0.66 us (2%)
    pallas_call x1, Pallas kernels, shards(): pl.pallas_call(functools.partial(kernel, dp, pairs, length, hard), name='...  28.6 us
    unnamed x1, local copies, waits for them, and re-layouts  0.66 us

profile of v3, /device:TPU:0, one launch (start us, length us, event | category | flops | bytes accessed | tf_op | source)
XLA Modules:
  0.0 31.7 jit_solution(10876988002401202896)
XLA Ops:
  1.3 28.6 %gradcache_step.1 = (f32[48,768]{1,0:T(8,128)S(1)}, f32[1,1]{1,0:T(1,128)S(1)}) custom-call(bf16[128,768]{1,0:T(8,128)(2,1)} %bitcast.8, bf16[128,768]{1,0:T(8,128)(2,1)} %bitcast.9, bf16[4,2,2,2,48,768]{5,4,3,2,1,0:T(8,128)(2,1)} %bitcast.6, bf16[4,2,2,2,48,768]{5,4,3,2,1,0:T(8,128)(2,1)} %bitcast.7, s32[1,1]{1,0:T(1,128)S(6)} %copy.12.pos_ref, s32[1,2]{1,0:T(1,128)} %bitcast.10), custom_call_target="tpu_custom_call" | custom-call | tf_op jit(solution)/shard_map/gradcache_step/pallas_call | solution.py:433
  30.0 0.7 %copy.10 = f32[48,768]{1,0:T(8,128)} copy(f32[48,768]{1,0:T(8,128)S(1)} %get-tuple-element.6) | data formatting | bytes 294912

commit v4 on v3

--- a/solution.py
+++ b/solution.py
@@ -263,12 +263,15 @@
         return pl.ds(sub * ROW_TILE, ROW_TILE)
 
     def turn(step):
-        own_turn = (step + 1) // depth
-        upper = (2 * layer) // depth
-        mirrored = upper * layer + (1 - upper) * (depth - 1 - layer)
-        place = step + (step - mirrored + depth) // depth
-        place = upper * place + (1 - upper) * (depth - 1 - place)
-        return own_turn * layer + (1 - own_turn) * place
+        short = jnp.minimum(layer, depth - 1 - layer)
+        ahead_first = jnp.where(2 * layer < depth, 1, -1)
+        lone = depth - 1 - 2 * short
+        late = jnp.maximum(step - lone, 0)
+        return jnp.where(
+            step < lone,
+            layer + ahead_first * (depth - 1 - short - step),
+            layer + ahead_first * (short - late // 2) * (2 * lax.rem(late, 2) - 1),
+        )
 
     def place_of(index):
         if strips == 1:
@@ -359,7 +362,8 @@
     steps = depth * strips
     moved = steps - strips
     lag_one, lag_two = LAGS
-    early = min(depth, -(-lag_one // strips))
+    early = min(depth, lag_one // strips)
+    sent = min(steps, lag_one)
 
     def backward_and_send(step):
         backward(step)
@@ -369,7 +373,7 @@
     loop(early, backward_and_send)
     loss_copy(my_rep).start()
     loop(depth - early, lambda step: backward(step + early))
-    sent = early * strips
+    loop(sent - early * strips, lambda step: send_first(early * strips + step))
     pipeline([
         (send_first, sent, steps, sent),
         (stage_two, 0, steps, 0),
@@ -381,6 +385,8 @@
         landed = z_in.at[pl.ds(0, depth - 1)]
         return remote(landed, landed, z_send.at[0], z_recv.at[0], (opposite, my_rep))
 
+    loss_copy(other_rep).wait_recv()
+    loss_ref[0, 0] = (losses[0] + losses[1])[0, 0] * (1.0 / (dp * pairs * 2))
     all_layers().wait_recv()
 
     def collect(step):
@@ -388,9 +394,6 @@
         out_ref[...] += z_in[source].astype(F32)
 
     loop(depth - 1, collect)
-
-    loss_copy(other_rep).wait_recv()
-    loss_ref[...] = (losses[0] + losses[1])[:, 0:1] * (1.0 / (dp * pairs * 2))
 
     all_indices().wait_send()
     all_embeds().wait_send()
@@ -435,10 +438,10 @@
         name="gradcache_step",
         out_shape=(
             pltpu.VMEM((rows, features), F32),
-            pltpu.VMEM((1, 1), F32),
+            pltpu.SMEM((1, 1), F32),
         ),
         in_specs=[hbm] * 4 + [fixed] * 2,
-        out_specs=(vmem, vmem),
+        out_specs=(vmem, pl.BlockSpec(memory_space=pltpu.SMEM)),
         scratch_shapes=[
             pltpu.VMEM((depth, 2, 2, 2, rows, features), BF16),
             pltpu.VMEM((depth, 2, 2, 2, rows, features), BF16),

time: 31.9 us -> 30.5 us (0.956)
  Pallas kernels: 28.6 us -> 27.9 us
  between operations: 2.45 us -> 1.8 us
    pallas_call x1, Pallas kernels: 28.6 us -> 27.9 us  [shards(): pl.pallas_call(functools.partial(kernel, dp, pairs, length, hard), name='...]
where the time goes in v4:
time: 30.5 us; the launch traced here: 30.4 us
  Pallas kernels  27.9 us (91%)
  between operations  1.8 us (6%)
  local copies, waits for them, and re-layouts  0.66 us (2%)
    pallas_call x1, Pallas kernels, shards(): pl.pallas_call(functools.partial(kernel, dp, pairs, length, hard), name='...  27.9 us
    unnamed x1, local copies, waits for them, and re-layouts  0.66 us

profile of v4, /device:TPU:0, one launch (start us, length us, event | category | flops | bytes accessed | tf_op | source)
XLA Modules:
  0.0 30.4 jit_solution(11914638999230698618)
XLA Ops:
  1.3 27.9 %gradcache_step.1 = (f32[48,768]{1,0:T(8,128)S(1)}, f32[1,1]{1,0:T(1,128)S(4)}) custom-call(bf16[128,768]{1,0:T(8,128)(2,1)} %bitcast.8, bf16[128,768]{1,0:T(8,128)(2,1)} %bitcast.9, bf16[4,2,2,2,48,768]{5,4,3,2,1,0:T(8,128)(2,1)} %bitcast.6, bf16[4,2,2,2,48,768]{5,4,3,2,1,0:T(8,128)(2,1)} %bitcast.7, s32[1,1]{1,0:T(1,128)S(6)} %copy.12.pos_ref, s32[1,2]{1,0:T(1,128)} %bitcast.10), custom_call_target="tpu_custom_call" | custom-call | tf_op jit(solution)/shard_map/gradcache_step/pallas_call | solution.py:436
  29.7 0.7 %copy.10 = f32[48,768]{1,0:T(8,128)} copy(f32[48,768]{1,0:T(8,128)S(1)} %get-tuple-element.6) | data formatting | bytes 294912

commit v5 on v4

--- a/solution.py
+++ b/solution.py
@@ -55,9 +55,9 @@
     dp, pairs, length, hard,
     q_ref, p_ref, up_ref, down_ref, pos_ref, hard_ref,
     out_ref, loss_ref,
-    up, down, tokens, hidden, normed, scales, slope, mixed, grads, slots, index_slots, every, index_rows,
+    up, down, tokens, normed, scales, slope, mixed, grads, slots, every, index_rows,
     first_out, first_in, first_kept, second_out, second_in, second_kept, z_out, z_in, losses,
-    pos_smem, hard_smem, t_sem, w_sem, d_send, d_recv, i_send, i_recv, e_send, e_recv,
+    pos_smem, hard_smem, t_sem, w_sem, d_send, d_recv, e_send, e_recv,
     l_send, l_recv, first_send, first_recv, second_send, second_recv, z_send, z_recv,
 ):
     depth = dp // 4
@@ -116,36 +116,11 @@
     pl.semaphore_signal(barrier, inc=1, device_id=(me, other_rep), device_id_type=MESH)
 
     every[...] = jnp.zeros_like(every)
-    index_rows[...] = jnp.full(index_rows.shape, -1, jnp.int32)
+    index_rows[...] = jnp.full(index_rows.shape, -1.0, F32)
 
     load_q.wait()
     load_p.wait()
     own = tokens[core]
-
-    def forward(step):
-        pre = dot_nt(own, up[pl.ds(step * span, span)].reshape(span * chunk, features))
-        columns = pl.ds(pl.multiple_of(step * span * chunk, span * chunk), span * chunk)
-        hidden[:, columns] = (pre * phi(pre)).astype(BF16)
-
-    span = 2 - depth % 2
-    loop(depth, lambda step: load(0, step).wait())
-    loop(depth // span, forward)
-    loop(depth, lambda step: load(1, step).wait())
-    summed = own.astype(F32) + jnp.dot(
-        hidden[...], down[...].reshape(depth * chunk, features), preferred_element_type=F32
-    )
-
-    means = []
-    for seq in range(seqs):
-        place = pl.ds(seq * length, length)
-        part = summed[seq * length:(seq + 1) * length]
-        centred = part - jnp.mean(part, -1, keepdims=True)
-        scale = lax.rsqrt(jnp.mean(centred * centred, -1, keepdims=True) + norm_eps)
-        unit = centred * scale
-        normed[core, place, :] = unit.astype(BF16)
-        scales[core, :, place] = jnp.broadcast_to(scale, (length, LANES)).T[0:8]
-        means.append(jnp.mean(unit, 0, keepdims=True))
-    slots[me] = jnp.concatenate(means, 0).astype(BF16)
 
     load_pos.wait()
     load_hard.wait()
@@ -158,7 +133,34 @@
             message = jnp.where(
                 (row_ids == row) & (lane_ids == 1 + pick), hard_smem[row, pick], message
             )
-    index_slots[me] = message
+    slots[me, :, features:] = message.astype(F32).astype(BF16)
+
+    halves = (slice(0, depth // 2), slice(depth // 2, depth))
+
+    def gelu_of(part):
+        pre = dot_nt(own, up[part].reshape(-1, features))
+        return (pre * phi(pre)).astype(BF16)
+
+    loop(depth, lambda step: load(0, step).wait())
+    loop(depth, lambda step: load(1, step).wait())
+    lows = [gelu_of(part) for part in halves]
+    summed = own.astype(F32)
+    for part, low_part in zip(halves, lows):
+        summed += jnp.dot(
+            low_part, down[part].reshape(-1, features), preferred_element_type=F32
+        )
+
+    means, units, scale_list = [], [], []
+    for seq in range(seqs):
+        place = pl.ds(seq * length, length)
+        part = summed[seq * length:(seq + 1) * length]
+        centred = part - jnp.mean(part, -1, keepdims=True)
+        scale = lax.rsqrt(jnp.mean(centred * centred, -1, keepdims=True) + norm_eps)
+        unit = centred * scale
+        units.append(unit)
+        scale_list.append(scale)
+        means.append(jnp.mean(unit, 0, keepdims=True))
+    slots[me, :, :features] = jnp.concatenate(means, 0).astype(BF16)
 
     pl.semaphore_wait(barrier, dp)
 
@@ -168,14 +170,12 @@
             (ahead(step + 1), my_rep),
         )
 
-    def index_copy(step):
-        return remote(
-            index_slots.at[me], index_slots.at[me], i_send.at[0], i_recv.at[0],
-            (ahead(step + 1), my_rep),
-        )
-
     loop(dp - 1, lambda step: embed_copy(step).start())
-    loop(dp - 1, lambda step: index_copy(step).start())
+
+    for seq in range(seqs):
+        place = pl.ds(seq * length, length)
+        normed[core, place, :] = units[seq].astype(BF16)
+        scales[core, :, place] = jnp.broadcast_to(scale_list[seq], (length, LANES)).T[0:8]
 
     def twin_copy(which, slot):
         ref = (tokens, normed, scales)[which].at[slot]
@@ -195,19 +195,14 @@
         twin_copy(which, 1 - core).wait_recv()
     loop(depth, lambda step: mix(step, 1 - core))
 
-    def all_indices():
-        landed = index_slots.at[pl.ds(0, dp - 1)]
-        return remote(landed, landed, i_send.at[0], i_recv.at[0], (me, my_rep))
-
     def all_embeds():
         landed = slots.at[pl.ds(0, dp - 1)]
         return remote(landed, landed, e_send.at[0], e_recv.at[0], (me, my_rep))
 
-    all_indices().wait_recv()
     all_embeds().wait_recv()
     for slot in range(dp):
-        every[slot * seqs:(slot + 1) * seqs, :] = slots[slot].astype(F32)
-        index_rows[slot * seqs:(slot + 1) * seqs, :] = index_slots[slot]
+        every[slot * seqs:(slot + 1) * seqs, :] = slots[slot, :, :features].astype(F32)
+        index_rows[slot * seqs:(slot + 1) * seqs, :] = slots[slot, :, features:].astype(F32)
 
     embeds = every[...].astype(BF16)
     scores = dot_nt(embeds, embeds)
@@ -219,7 +214,7 @@
         (row < dp * seqs) & (row_place < pairs) & (column < dp * seqs) & (column_place >= pairs)
     )
     passage = (column // seqs) * pairs + column_place - pairs
-    indices = index_rows[...]
+    indices = index_rows[...].astype(jnp.int32)
     target = valid & (passage == indices[:, 0:1])
     is_hard = passage == indices[:, 1:2]
     for pick in range(1, hard):
@@ -367,12 +362,20 @@
 
     def backward_and_send(step):
         backward(step)
-        for sub in range(strips):
-            send_first(step * strips + sub)
+
+        @pl.when(core == 0)
+        def send_now():
+            for sub in range(strips):
+                send_first(step * strips + sub)
 
     loop(early, backward_and_send)
     loss_copy(my_rep).start()
     loop(depth - early, lambda step: backward(step + early))
+
+    @pl.when(core != 0)
+    def send_later():
+        loop(early * strips, send_first)
+
     loop(sent - early * strips, lambda step: send_first(early * strips + step))
     pipeline([
         (send_first, sent, steps, sent),
@@ -395,7 +398,6 @@
 
     loop(depth - 1, collect)
 
-    all_indices().wait_send()
     all_embeds().wait_send()
     for which in range(3):
         twin_copy(which, core).wait_send()
@@ -410,6 +412,7 @@
 
 def shards(dp, rep, q_hidden, p_hidden, w_up, w_down, pos_index, hard_index):
     assert rep == 2 and dp % 4 == 0
+    assert dp * q_hidden.shape[1] <= 256
     pairs, length, features = q_hidden.shape[1:]
     hard = hard_index.shape[-1]
     hidden_units = w_up.shape[0]
@@ -446,16 +449,14 @@
             pltpu.VMEM((depth, 2, 2, 2, rows, features), BF16),
             pltpu.VMEM((depth, 2, 2, 2, rows, features), BF16),
             pltpu.VMEM((2, count, features), BF16),
-            pltpu.VMEM((count, depth * chunk), BF16),
             pltpu.VMEM((2, count, features), BF16),
             pltpu.VMEM((2, 8, count), F32),
             pltpu.VMEM((2, depth, 4 * rows, count), F32),
             pltpu.VMEM((2, depth, 4 * rows, count), F32),
             pltpu.VMEM((4 * rows, 2 * count), BF16),
-            pltpu.VMEM((dp, seqs, features), BF16),
-            pltpu.VMEM((dp, seqs, LANES), jnp.int32),
+            pltpu.VMEM((dp, seqs, features + LANES), BF16),
             pltpu.VMEM((padded, features), F32),
-            pltpu.VMEM((padded, LANES), jnp.int32),
+            pltpu.VMEM((padded, LANES), F32),
             pltpu.VMEM((depth, 2, 2, rows, half), BF16),
             pltpu.VMEM((depth, 2, 2, rows, half), BF16),
             pltpu.VMEM((depth, 2, 2, rows, half), F32),
@@ -467,7 +468,7 @@
             pltpu.VMEM((2, 1, LANES), F32),
             pltpu.SMEM((1, pairs), jnp.int32), pltpu.SMEM((pairs, hard), jnp.int32),
             dma((4,)), dma((2, depth)),
-            dma((3,)), dma((3,)), dma((1,)), dma((1,)), dma((1,)), dma((1,)),
+            dma((3,)), dma((3,)), dma((1,)), dma((1,)),
             dma((1,)), dma((1,)),
             dma((2,)), dma((depth, strips, 2)), dma((2,)), dma((depth, strips, 2)),
             dma((1,)), dma((1,)),

time: 30.5 us -> 29.9 us (0.980)
  Pallas kernels: 27.9 us -> 27.1 us
    pallas_call x1, Pallas kernels: 27.9 us -> 27.1 us  [shards(): pl.pallas_call(functools.partial(kernel, dp, pairs, length, hard), name='...]
where the time goes in v5:
time: 29.9 us; the launch traced here: 29.6 us
  Pallas kernels  27.1 us (91%)
  between operations  1.8 us (6%)
  local copies, waits for them, and re-layouts  0.66 us (2%)
    pallas_call x1, Pallas kernels, shards(): pl.pallas_call(functools.partial(kernel, dp, pairs, length, hard), name='...  27.1 us
    unnamed x1, local copies, waits for them, and re-layouts  0.66 us

profile of v5, /device:TPU:0, one launch (start us, length us, event | category | flops | bytes accessed | tf_op | source)
XLA Modules:
  0.0 29.6 jit_solution(724114963743544216)
XLA Ops:
  1.3 27.1 %gradcache_step.1 = (f32[48,768]{1,0:T(8,128)S(1)}, f32[1,1]{1,0:T(1,128)S(4)}) custom-call(bf16[128,768]{1,0:T(8,128)(2,1)} %bitcast.8, bf16[128,768]{1,0:T(8,128)(2,1)} %bitcast.9, bf16[4,2,2,2,48,768]{5,4,3,2,1,0:T(8,128)(2,1)} %bitcast.6, bf16[4,2,2,2,48,768]{5,4,3,2,1,0:T(8,128)(2,1)} %bitcast.7, s32[1,1]{1,0:T(1,128)S(6)} %copy.12.pos_ref, s32[1,2]{1,0:T(1,128)} %bitcast.10), custom_call_target="tpu_custom_call" | custom-call | tf_op jit(solution)/shard_map/gradcache_step/pallas_call | solution.py:439
  28.9 0.7 %copy.10 = f32[48,768]{1,0:T(8,128)} copy(f32[48,768]{1,0:T(8,128)S(1)} %get-tuple-element.6) | data formatting | bytes 294912

commit v6 on v5

--- a/solution.py
+++ b/solution.py
@@ -377,9 +377,14 @@
         loop(early * strips, send_first)
 
     loop(sent - early * strips, lambda step: send_first(early * strips + step))
+    def finish_loss(index):
+        loss_copy(other_rep).wait_recv()
+        loss_ref[0, 0] = (losses[0] + losses[1])[0, 0] * (1.0 / (dp * pairs * 2))
+
     pipeline([
+        (stage_two, 0, steps, 0),
         (send_first, sent, steps, sent),
-        (stage_two, 0, steps, 0),
+        (finish_loss, 0, 1, -lag_two),
         (lambda index: stage_three(index, False), 0, moved, -lag_two),
         (lambda index: stage_three(index, True), moved, steps, -lag_two),
     ])
@@ -388,15 +393,18 @@
         landed = z_in.at[pl.ds(0, depth - 1)]
         return remote(landed, landed, z_send.at[0], z_recv.at[0], (opposite, my_rep))
 
-    loss_copy(other_rep).wait_recv()
-    loss_ref[0, 0] = (losses[0] + losses[1])[0, 0] * (1.0 / (dp * pairs * 2))
     all_layers().wait_recv()
 
-    def collect(step):
-        source = lax.rem(layer + depth - 1 - step, depth)
-        out_ref[...] += z_in[source].astype(F32)
-
-    loop(depth - 1, collect)
+    def arrived(step):
+        return z_in[lax.rem(layer + depth - 1 - step, depth)].astype(F32)
+
+    if depth <= 16:
+        out_ref[...] += sum(arrived(step) for step in range(depth - 1))
+    else:
+        def collect(step):
+            out_ref[...] += arrived(step)
+
+        loop(depth - 1, collect)
 
     all_embeds().wait_send()
     for which in range(3):

time: 29.9 us -> 29.9 us (level)
  no operation moved by 1% of the time
where the time goes in v6:
time: 29.9 us; the launch traced here: 29.7 us
  Pallas kernels  27.3 us (91%)
  between operations  1.8 us (6%)
  local copies, waits for them, and re-layouts  0.66 us (2%)
    pallas_call x1, Pallas kernels, shards(): pl.pallas_call(functools.partial(kernel, dp, pairs, length, hard), name='...  27.3 us
    unnamed x1, local copies, waits for them, and re-layouts  0.66 us

profile of v6, /device:TPU:0, one launch (start us, length us, event | category | flops | bytes accessed | tf_op | source)
XLA Modules:
  0.0 29.7 jit_solution(15601231481583883571)
XLA Ops:
  1.3 27.3 %gradcache_step.1 = (f32[48,768]{1,0:T(8,128)S(1)}, f32[1,1]{1,0:T(1,128)S(4)}) custom-call(bf16[128,768]{1,0:T(8,128)(2,1)} %bitcast.8, bf16[128,768]{1,0:T(8,128)(2,1)} %bitcast.9, bf16[4,2,2,2,48,768]{5,4,3,2,1,0:T(8,128)(2,1)} %bitcast.6, bf16[4,2,2,2,48,768]{5,4,3,2,1,0:T(8,128)(2,1)} %bitcast.7, s32[1,1]{1,0:T(1,128)S(6)} %copy.12.pos_ref, s32[1,2]{1,0:T(1,128)} %bitcast.10), custom_call_target="tpu_custom_call" | custom-call | tf_op jit(solution)/shard_map/gradcache_step/pallas_call | solution.py:447
  29.1 0.7 %copy.10 = f32[48,768]{1,0:T(8,128)} copy(f32[48,768]{1,0:T(8,128)S(1)} %get-tuple-element.6) | data formatting | bytes 294912

commit v7 on v5

--- a/solution.py
+++ b/solution.py
@@ -137,15 +137,15 @@
 
     halves = (slice(0, depth // 2), slice(depth // 2, depth))
 
-    def gelu_of(part):
-        pre = dot_nt(own, up[part].reshape(-1, features))
-        return (pre * phi(pre)).astype(BF16)
+    def up_of(part):
+        return dot_nt(own, up[part].reshape(-1, features))
 
     loop(depth, lambda step: load(0, step).wait())
     loop(depth, lambda step: load(1, step).wait())
-    lows = [gelu_of(part) for part in halves]
+    pres = [up_of(part) for part in halves]
     summed = own.astype(F32)
-    for part, low_part in zip(halves, lows):
+    for part, pre in zip(halves, pres):
+        low_part = (pre * phi(pre)).astype(BF16)
         summed += jnp.dot(
             low_part, down[part].reshape(-1, features), preferred_element_type=F32
         )

time: 29.9 us -> 29.9 us (level)
  no operation moved by 1% of the time
where the time goes in v7:
time: 29.9 us; the launch traced here: 29.6 us
  Pallas kernels  27.1 us (91%)
  between operations  1.8 us (6%)
  local copies, waits for them, and re-layouts  0.66 us (2%)
    pallas_call x1, Pallas kernels, shards(): pl.pallas_call(functools.partial(kernel, dp, pairs, length, hard), name='...  27.1 us
    unnamed x1, local copies, waits for them, and re-layouts  0.66 us

profile of v7, /device:TPU:0, one launch (start us, length us, event | category | flops | bytes accessed | tf_op | source)
XLA Modules:
  0.0 29.6 jit_solution(724114963743544216)
XLA Ops:
  1.3 27.1 %gradcache_step.1 = (f32[48,768]{1,0:T(8,128)S(1)}, f32[1,1]{1,0:T(1,128)S(4)}) custom-call(bf16[128,768]{1,0:T(8,128)(2,1)} %bitcast.8, bf16[128,768]{1,0:T(8,128)(2,1)} %bitcast.9, bf16[4,2,2,2,48,768]{5,4,3,2,1,0:T(8,128)(2,1)} %bitcast.6, bf16[4,2,2,2,48,768]{5,4,3,2,1,0:T(8,128)(2,1)} %bitcast.7, s32[1,1]{1,0:T(1,128)S(6)} %copy.12.pos_ref, s32[1,2]{1,0:T(1,128)} %bitcast.10), custom_call_target="tpu_custom_call" | custom-call | tf_op jit(solution)/shard_map/gradcache_step/pallas_call | solution.py:439
  28.9 0.7 %copy.10 = f32[48,768]{1,0:T(8,128)} copy(f32[48,768]{1,0:T(8,128)S(1)} %get-tuple-element.6) | data formatting | bytes 294912
